TPU v7x, 32 devices: a whole 2x2x4 slice. The times are simulated.
32 devices in a mesh: groups: 2 (over x), row: 8 (over z, y), head: 2 (over core).
Axes of the slice: x: 2, y: 2, z: 4, core: 2. Of those that a mesh axis runs over, the one named last changes fastest.
Arguments:
- hidden: bfloat16 [48, 4096], P('groups'), parts along dimension 0, may hold values from -6 to 6
- norm_gain: float32 [4096], replicated, may hold values from 0.1 to 1.9
- w_query: bfloat16 [8, 256, 4096], P('head', 'row'), may hold values from -0.09375 to 0.09375
- w_key: bfloat16 [8, 256, 4096], P('head', 'row'), may hold values from -0.09375 to 0.09375
- w_value: bfloat16 [8, 512, 4096], P('head', 'row'), may hold values from -0.09375 to 0.09375
- w_outgate: bfloat16 [8, 512, 4096], P('head', 'row'), may hold values from -0.09375 to 0.09375
- w_out: bfloat16 [8, 512, 4096], P('head', 'row'), may hold values from -0.125 to 0.125
- w_gates: bfloat16 [2, 8, 4096], P(None, 'head'), may hold values from -0.09375 to 0.09375
- gate_bias: float32 [2, 8], P(None, 'head'), may hold values from -2 to 4
- headnorm_gain: float32 [8, 512], P('head', 'row'), may hold values from 0.1 to 1.9
- final_gain: float32 [4096], replicated, may hold values from 0.1 to 1.9
- w_vocab: bfloat16 [25152, 4096], P(('row', 'head')), may hold values from -39.0625 to 39.0625
- memory: float32 [48, 8, 256, 512], P('groups', 'head', 'row'), parts along dimension 0, may hold values from -6 to 6
- normalizer: float32 [48, 8, 256], P('groups', 'head', 'row'), parts along dimension 0, may hold values from -6 to 6
- stabilizer: float32 [48, 8], P('groups', 'head'), parts along dimension 0, may hold values from -2 to 2
- targets: int32 [48], P('groups'), parts along dimension 0, may hold values from 0 to 25151
Outputs:
- memory_out: float32 [48, 8, 256, 512], P('groups', 'head', 'row'), parts along dimension 0
- normalizer_out: float32 [48, 8, 256], P('groups', 'head', 'row'), parts along dimension 0
- stabilizer_out: float32 [48, 8], P('groups', 'head'), parts along dimension 0
- hidden_out: bfloat16 [48, 4096], P('groups', ('row', 'head')), parts along dimension 0
- log_prob: float32 [48], P('groups'), parts along dimension 0
There are 2 independent parts, one for each index of `groups`. A program takes and returns all parts, laid end to end along the dimension named above; an argument that names none is the same for every part. Nothing has to cross between parts.
All inputs are finite; a program needn't handle non-finite values.
Results may differ from a plain program's by a relative error of at most 0.0035.
The roundings to bfloat16 on the way count: a program that leaves them out, or rounds other values in their place, can miss the bound.
Values may be sent and summed in bfloat16 or wider, within the bound.
A program may use at most 64 MiB of HBM per device.

v0:
```python
import math
import jax
import jax.numpy as jnp
from jax import lax
from jax.sharding import PartitionSpec as P

QK_DIM = 256
epsilon = 1e-06


def joined_2(value, axis, join):
    pieces = jax.tree.map(lambda part: lax.all_gather(part, axis), value)
    head = jax.tree.map(lambda part: part[0], pieces)
    tail = jax.tree.map(lambda part: part[1:], pieces)
    total, _ = lax.scan(lambda total, share: (join(total, share), None), head, tail)
    return total


def rms_round(stream, gain):
    scale = lax.rsqrt(jnp.mean(stream * stream, axis=-1, keepdims=True) + epsilon)
    return (stream * scale * gain).astype(jnp.bfloat16)


def per_device(
    hidden,
    norm_gain,
    w_query,
    w_key,
    w_value,
    w_outgate,
    w_out,
    w_gates,
    gate_bias,
    headnorm_gain,
    final_gain,
    w_vocab,
    memory,
    normalizer,
    stabilizer,
    targets,
):
    value_rows = w_value.shape[1]
    stream = hidden.astype(jnp.float32)
    normed_in = rms_round(stream, norm_gain)

    def project(weights):
        return jnp.einsum("sd,hjd->shj", normed_in, weights, preferred_element_type=jnp.float32)

    queries = project(w_query) / math.sqrt(QK_DIM)
    key_part = project(w_key)
    value_part = project(w_value).astype(jnp.bfloat16)
    outgate_pre = project(w_outgate)
    gate_pre = (
        jnp.einsum("sd,ghd->gsh", normed_in, w_gates, preferred_element_type=jnp.float32)
        + gate_bias[:, None, :]
    )
    log_forget = jax.nn.log_sigmoid(gate_pre[1])
    stabilizer_out = jnp.maximum(log_forget + stabilizer, gate_pre[0])
    decay_rate = jnp.exp(log_forget + stabilizer - stabilizer_out)
    inflow = jnp.exp(gate_pre[0] - stabilizer_out)
    scaled_key = inflow[:, :, None] * key_part
    memory_out = (
        decay_rate[:, :, None, None] * memory
        + scaled_key[:, :, :, None]
        * lax.all_gather(value_part, "row", axis=2, tiled=True).astype(jnp.float32)[:, :, None, :]
    )
    normalizer_out = decay_rate[:, :, None] * normalizer + scaled_key
    partial_readout = jnp.einsum(
        "shj,shje->she", queries, memory_out, precision=lax.Precision.HIGHEST
    )
    readout = lax.psum(partial_readout, "row")
    average = jnp.mean(readout, axis=-1)
    centered_full = readout - average[:, :, None]
    variance = jnp.mean(centered_full * centered_full, axis=-1)
    centered = lax.dynamic_slice_in_dim(
        centered_full, lax.axis_index("row") * value_rows, value_rows, 2
    )
    normed = centered * lax.rsqrt(variance + epsilon)[:, :, None] * headnorm_gain
    gated_out = (jax.nn.sigmoid(outgate_pre) * normed).astype(jnp.bfloat16)
    partial_terms = jnp.einsum("shj,hjd->sd", gated_out, w_out, preferred_element_type=jnp.float32)
    position = lax.axis_index("row") * lax.axis_size("head") + lax.axis_index("head")
    share_width = hidden.shape[1] // (lax.axis_size("row") * lax.axis_size("head"))
    vocab_here = w_vocab.shape[0]
    projection = lax.psum(partial_terms, ("row", "head"))
    new_full = (stream + projection).astype(jnp.bfloat16)
    final_feat = rms_round(new_full.astype(jnp.float32), final_gain)
    logits = jnp.einsum("sd,vd->sv", final_feat, w_vocab, preferred_element_type=jnp.float32)
    hidden_out = lax.dynamic_slice_in_dim(new_full, position * share_width, share_width, 1)
    local_ids = targets - position * vocab_here
    is_target = jnp.arange(vocab_here, dtype=jnp.int32)[None, :] == local_ids[:, None]
    target_term = jnp.sum(jnp.where(is_target, logits, 0.0), axis=-1)
    local_max = jnp.max(logits, axis=-1)
    local_sum = jnp.sum(jnp.exp(logits - local_max[:, None]), axis=-1)

    def combine(earlier, later):
        highest = jnp.maximum(earlier[0], later[0])
        joined = earlier[1] * jnp.exp(earlier[0] - highest) + later[1] * jnp.exp(later[0] - highest)
        return (highest, joined, earlier[2] + later[2])

    highest, exp_total, picked = joined_2(
        (local_max, local_sum, target_term), ("row", "head"), combine
    )
    log_prob = picked - (highest + jnp.log(exp_total))
    return (memory_out, normalizer_out, stabilizer_out, hidden_out, log_prob)


def solution(mesh):
    in_specs = (
        P("groups", None),
        P(),
        P("head", "row", None),
        P("head", "row", None),
        P("head", "row", None),
        P("head", "row", None),
        P("head", "row", None),
        P(None, "head", None),
        P(None, "head"),
        P("head", "row"),
        P(),
        P(("row", "head"), None),
        P("groups", "head", "row", None),
        P("groups", "head", "row"),
        P("groups", "head"),
        P("groups"),
    )
    out_specs = (
        P("groups", "head", "row", None),
        P("groups", "head", "row"),
        P("groups", "head"),
        P("groups", ("row", "head")),
        P("groups"),
    )
    return jax.shard_map(
        per_device, mesh=mesh, in_specs=in_specs, out_specs=out_specs, check_vma=False
    )
```

profile of v0, /device:TPU:0, one launch (start us, length us, event | category | flops | bytes accessed | tf_op | source)
XLA Modules:
  0.0 280.0 jit_solution(1592682969917463788)
XLA Ops:
  7.2 1.2 fusion.17
  8.5 2.7 convolution_convert_fusion
  11.3 33.0 %all_gather.21 = bf16[24,4,512]{0,1,2:T(4,128)(2,1)S(1)} all-gather(bf16[24,4,64]{0,1,2:T(4,128)(2,1)S(1)} %copy.34), channel_id=1, replica_groups=mesh['groups'=2,'row'=8,'head'=2] {'row'}, dimensions={2}, use_global_device_ids=true | all-gather | bytes 110592 | tf_op jit(solution)/shard_map/all_gather | solution.py:65
  44.7 1.2 fusion.13
  45.9 0.7 subtract_exponential_fusion.1
  46.7 2.2 fusion.28
  48.9 2.2 fusion.7
  51.1 3.4 %multiply_add_fusion = f32[24,4,32,512]{3,2,1,0:T(8,128)S(1)} fusion(f32[24,4,32,512]{3,2,1,0:T(8,128)} %param.30, f32[24,4,512]{2,1,0:T(4,128)S(1)} %copy.36, f32[24,4,32]{2,1,0:T(4,128)S(1)} %copy.33, f32[24,4]{1,0:T(8,128)S(1)} %copy.32), kind=kLoop, calls=%fused_computation.10 | loop fusion | flops 4718592 | bytes 12792192 | tf_op jit(solution)/shard_map/add | solution.py:63
  54.5 2.7 copy-done.1
  57.2 3.1 %fusion.26 = f32[24,4,1,512]{3,2,1,0:T(1,128)S(1)} fusion(f32[24,4,32,512]{3,2,1,0:T(8,128)S(1)} %multiply_add_fusion, f32[24,4,32,1]{2,0,1,3:T(8,128)S(1)} %fusion.7), kind=kOutput, calls=%fused_computation.46 | convolution fusion | flops 18874368 | bytes 6500352 | tf_op jit(solution)/shard_map/shj,shje->she/dot_general | solution.py:68
  60.4 0.7 copy.47
  61.2 0.6 copy.38
  61.8 0.6 dynamic-slice
  63.1 70.0 %all-reduce.7.cloned.1.call-done = f32[24,4,512]{2,0,1:T(8,128)} async-done(((f32[24,4,512]{2,0,1:T(8,128)}), f32[24,4,512]{2,0,1:T(8,128)}) %all-reduce.7.cloned.1.call-update) | async-done | bytes 196624 | tf_op jit(solution)/shard_map/psum | solution.py:71
  133.1 1.0 reduce_sum.55
  134.1 1.1 multiply_reduce_fusion
  135.3 3.8 %convolution_bitcast_fusion = f32[24,4096]{1,0:T(8,128)} fusion(bf16[4,64,4096]{2,1,0:T(8,128)(2,1)S(1)} %copy-done, bf16[4,64,4096]{2,1,0:T(8,128)(2,1)} %param.23, f32[24,4,512]{2,0,1:T(8,128)S(1)} %get-tuple-element.86, s32[]{:T(128)S(6)} %select_n.16, f32[4,64]{1,0:T(4,128)S(1)} %copy-done.6, f32[24,4]{0,1:T(4,128)S(1)} %add_rsqrt_fusion, ...), kind=kOutput, calls=%fused_computation.11 | convolution fusion | flops 101099520 | bytes 4854276 | tf_op jit(solution)/shard_map/shj,hjd->sd/dot_general | solution.py:80
  139.1 90.6 %all-reduce.9.cloned.1.call-done = f32[24,4096]{1,0:T(8,128)} async-done(((f32[24,4096]{1,0:T(8,128)}), f32[24,4096]{1,0:T(8,128)}) %all-reduce.9.cloned.1.call-update) | async-done | bytes 393232 | tf_op jit(solution)/shard_map/psum | solution.py:84
  229.6 1.2 fusion.14
  230.8 8.3 %fusion.50 = (f32[24]{0:T(128)S(1)}, f32[24,1572]{1,0:T(8,128)S(1)}) fusion(bf16[1572,4096]{1,0:T(8,128)(2,1)} %param.29, bf16[24,4096]{1,0:T(8,128)(2,1)S(1)} %get-tuple-element.84, f32[4096]{0:T(1024)S(1)} %copy-done.4, f32[24]{0:T(128)S(1)} %add_rsqrt_fusion.1), kind=kOutput, calls=%fused_computation.74 | convolution fusion | flops 309498688 | bytes 13241920 | tf_op jit(solution)/shard_map/sd,vd->sv/dot_general | solution.py:87
  240.0 30.9 %all-reduce.3 = (f32[384]{0:T(512)S(1)}, f32[384]{0:T(512)S(1)}, f32[384]{0:T(512)S(1)}) all-reduce(f32[384]{0:T(512)S(1)} %dynamic-update-slice, f32[384]{0:T(512)S(1)} %dynamic-update-slice.1, f32[384]{0:T(512)S(1)} %dynamic-update-slice.2), channel_id=2, replica_groups=mesh['groups'=2,'row'=8,'head'=2] {'row','head'}, use_global_device_ids=true, to_apply=%add | all-reduce | flops 1152 | bytes 9216
  271.2 0.6 constant_dynamic-slice_fusion.3
  272.0 0.6 while.14
  272.7 0.5 add_subtract_fusion
  (63 shorter events, 2.6 us)
Async XLA Ops:
  7.2 128.1 %copy-start = (bf16[4,64,4096]{2,1,0:T(8,128)(2,1)S(1)}, bf16[4,64,4096]{2,1,0:T(8,128)(2,1)}, u32[]{:S(2)}) copy-start(bf16[4,64,4096]{2,1,0:T(8,128)(2,1)} %param.24) | copy-start | bytes 6291460
  7.2 125.9 %all-reduce.7.cloned.1.call-start = ((), (), s32[]{:S(2)}) async-start(), calls=%async_computation | async-start | bytes 393216 | tf_op jit(solution)/shard_map/psum | solution.py:71
  46.6 7.9 %copy-start.5 = (f32[24,4]{0,1:T(4,128)}, f32[24,4]{0,1:T(4,128)S(1)}, u32[]{:S(2)}) copy-start(f32[24,4]{0,1:T(4,128)S(1)} %get-tuple-element.88) | copy-start | bytes 1156
  54.5 2.7 copy-start.1
  57.2 4.6 %copy-start.8 = (u32[32]{0:T(128)S(1)}, u32[32]{0:T(128)}, u32[]{:S(2)}) copy-start(u32[32]{0:T(128)} %constant.57) | copy-start | bytes 388
  57.2 78.0 %copy-start.2 = (bf16[24,4096]{1,0:T(8,128)(2,1)S(1)}, bf16[24,4096]{1,0:T(8,128)(2,1)}, u32[]{:S(2)}) copy-start(bf16[24,4096]{1,0:T(8,128)(2,1)} %param.18) | copy-start | bytes 589828
  57.2 78.0 %copy-start.3 = (f32[4096]{0:T(1024)S(1)}, f32[4096]{0:T(1024)}, u32[]{:S(2)}) copy-start(f32[4096]{0:T(1024)} %param.19) | copy-start | bytes 49156
  57.2 78.1 %copy-start.6 = (f32[4,64]{1,0:T(4,128)S(1)}, f32[4,64]{1,0:T(4,128)}, u32[]{:S(2)}) copy-start(f32[4,64]{1,0:T(4,128)} %param.27) | copy-start | bytes 3076
  57.2 81.8 %copy-start.7 = (s32[24]{0:T(128)S(1)}, s32[24]{0:T(128)}, u32[]{:S(2)}) copy-start(s32[24]{0:T(128)} %param.33) | copy-start | bytes 292
  57.2 173.6 %copy-start.4 = (f32[4096]{0:T(1024)S(1)}, f32[4096]{0:T(1024)}, u32[]{:S(2)}) copy-start(f32[4096]{0:T(1024)} %param.28) | copy-start | bytes 49156
  61.1 168.5 %all-reduce.9.cloned.1.call-start = ((), (), s32[]{:S(2)}) async-start(), calls=%async_computation.1 | async-start | bytes 786432 | tf_op jit(solution)/shard_map/psum | solution.py:84
Sparse Core Ops, SparseCore 0:
  61.2 71.7 all-reduce.6
  139.2 90.4 all-reduce.8
where the time goes:
time: 281 us; the launch traced here: 280 us
  waiting for transfers between devices  161 us (57%)
  blocking collectives  64 us (23%)
  matrix products  23.4 us (8%)
  between operations  15 us (5%)
  other arithmetic  9.78 us (3%)
  local copies, waits for them, and re-layouts  7.02 us (2%)
    psum x1, waiting for transfers between devices, per_device(): projection = lax.psum(partial_terms, ('row', 'head'))  90.6 us
    psum x1, waiting for transfers between devices, per_device(): readout = lax.psum(partial_readout, 'row')  70 us
    all_gather x1, blocking collectives, per_device(): lax.all_gather(value_part, 'row', axis=2, tiled=True).astype(jnp.float32)  33 us
    unnamed x1, blocking collectives  30.9 us
    dot_general x1, matrix products, per_device(): jnp.einsum('sd,vd->sv', final_feat, w_vocab, preferred_element_type=jnp.f...  8.26 us
    dot_general x3, matrix products, project(): jnp.einsum('sd,hjd->shj', normed_in, weights, preferred_element_type=jnp....  7.03 us
  transfers between devices with their start and end apart: 2, of which 2 were waited for; matrix products, arithmetic and copies ran while one was open for 0% of the time, Pallas kernels for 0%

commit v1 on v0

--- a/solution.py
+++ b/solution.py
@@ -81,7 +81,8 @@
     position = lax.axis_index("row") * lax.axis_size("head") + lax.axis_index("head")
     share_width = hidden.shape[1] // (lax.axis_size("row") * lax.axis_size("head"))
     vocab_here = w_vocab.shape[0]
-    projection = lax.psum(partial_terms, ("row", "head"))
+    next_value = lax.all_gather(partial_terms, axis_name=("row", "head"))
+    projection = jnp.sum(next_value, axis=0)
     new_full = (stream + projection).astype(jnp.bfloat16)
     final_feat = rms_round(new_full.astype(jnp.float32), final_gain)
     logits = jnp.einsum("sd,vd->sv", final_feat, w_vocab, preferred_element_type=jnp.float32)

time: 281 us -> 254 us (0.904)
  waiting for transfers between devices: 161 us -> 131 us
    psum x1 -> x0, waiting for transfers between devices: 90.6 us -> none  [per_device(): projection = lax.psum(partial_terms, ('row', 'head'))]
    all_gather x0 -> x1, waiting for transfers between devices: none -> 58.7 us  [per_device(): next_value = lax.all_gather(partial_terms, axis_name=('row', 'head'))]
    reduce_sum x0 -> x1, other arithmetic: none -> 3.11 us  [per_device(): projection = jnp.sum(next_value, axis=0)]
where the time goes in v1:
time: 254 us; the launch traced here: 253 us
  waiting for transfers between devices  131 us (52%)
  blocking collectives  64.9 us (26%)
  matrix products  23.4 us (9%)
  between operations  15 us (6%)
  other arithmetic  11.9 us (5%)
  local copies, waits for them, and re-layouts  7.02 us (3%)
    psum x1, waiting for transfers between devices, per_device(): readout = lax.psum(partial_readout, 'row')  71.9 us
    all_gather x1, waiting for transfers between devices, per_device(): next_value = lax.all_gather(partial_terms, axis_name=('row', 'head'))  58.7 us
    all_gather x1, blocking collectives, per_device(): lax.all_gather(value_part, 'row', axis=2, tiled=True).astype(jnp.float32)  33 us
    unnamed x1, blocking collectives  31.8 us
    dot_general x1, matrix products, per_device(): jnp.einsum('sd,vd->sv', final_feat, w_vocab, preferred_element_type=jnp.f...  8.26 us
    dot_general x3, matrix products, project(): jnp.einsum('sd,hjd->shj', normed_in, weights, preferred_element_type=jnp....  7.03 us
  transfers between devices with their start and end apart: 2, of which 2 were waited for; matrix products, arithmetic and copies ran while one was open for 0% of the time, Pallas kernels for 0%

profile of v1, /device:TPU:0, one launch (start us, length us, event | category | flops | bytes accessed | tf_op | source)
XLA Modules:
  0.0 253.1 jit_solution(13840420870915833634)
XLA Ops:
  7.2 1.2 fusion.17
  8.5 2.7 %convolution_convert_fusion = bf16[24,4,64]{2,0,1:T(8,128)(2,1)S(1)} fusion(bf16[4,64,4096]{2,1,0:T(8,128)(2,1)} %param.22, bf16[24,4096]{1,0:T(8,128)(2,1)} %param.18, f32[4096]{0:T(1024)} %param.19, f32[24]{0:T(128)S(1)} %add_rsqrt_fusion.2), kind=kOutput, calls=%fused_computation.21 | convolution fusion | flops 50731008 | bytes 2322528 | tf_op jit(solution)/shard_map/sd,hjd->shj/dot_general | solution.py:47
  11.3 33.0 %all_gather.27 = bf16[24,4,512]{0,1,2:T(4,128)(2,1)S(1)} all-gather(bf16[24,4,64]{0,1,2:T(4,128)(2,1)S(1)} %copy.34), channel_id=1, replica_groups=mesh['groups'=2,'row'=8,'head'=2] {'row'}, dimensions={2}, use_global_device_ids=true | all-gather | bytes 110592 | tf_op jit(solution)/shard_map/all_gather | solution.py:65
  44.7 1.2 fusion.13
  45.9 0.7 subtract_exponential_fusion.1
  46.7 2.2 fusion.28
  48.9 2.2 fusion.7
  51.1 3.4 %multiply_add_fusion = f32[24,4,32,512]{3,2,1,0:T(8,128)S(1)} fusion(f32[24,4,32,512]{3,2,1,0:T(8,128)} %param.30, f32[24,4,512]{2,1,0:T(4,128)S(1)} %copy.36, f32[24,4,32]{2,1,0:T(4,128)S(1)} %copy.33, f32[24,4]{1,0:T(8,128)S(1)} %copy.32), kind=kLoop, calls=%fused_computation.10 | loop fusion | flops 4718592 | bytes 12792192 | tf_op jit(solution)/shard_map/add | solution.py:63
  54.5 2.7 %copy-done.1 = f32[24,4,32,512]{3,2,1,0:T(8,128)} copy-done((f32[24,4,32,512]{3,2,1,0:T(8,128)}, f32[24,4,32,512]{3,2,1,0:T(8,128)S(1)}, u32[]{:S(2)}) %copy-start.1) | copy-done | bytes 6291480
  57.2 3.1 %fusion.26 = f32[24,4,1,512]{3,2,1,0:T(1,128)S(1)} fusion(f32[24,4,32,512]{3,2,1,0:T(8,128)S(1)} %multiply_add_fusion, f32[24,4,32,1]{2,0,1,3:T(8,128)S(1)} %fusion.7), kind=kOutput, calls=%fused_computation.46 | convolution fusion | flops 18874368 | bytes 6500352 | tf_op jit(solution)/shard_map/shj,shje->she/dot_general | solution.py:68
  60.3 0.7 copy.47
  61.2 71.9 %all-reduce.6.cloned.1.call-done = f32[24,4,512]{2,0,1:T(8,128)} async-done(((f32[24,4,512]{2,0,1:T(8,128)}), f32[24,4,512]{2,0,1:T(8,128)}) %all-reduce.6.cloned.1.call-update) | async-done | bytes 196624 | tf_op jit(solution)/shard_map/psum | solution.py:71
  133.1 1.0 reduce_sum.64
  134.1 1.1 multiply_reduce_fusion
  135.3 3.8 %convolution_bitcast_fusion = f32[24,4096]{1,0:T(8,128)} fusion(bf16[4,64,4096]{2,1,0:T(8,128)(2,1)S(1)} %copy-done, bf16[4,64,4096]{2,1,0:T(8,128)(2,1)} %param.23, f32[24,4,512]{2,0,1:T(8,128)S(1)} %get-tuple-element.86, s32[]{:T(128)S(6)} %select_n.16, f32[4,64]{1,0:T(4,128)S(1)} %copy-done.6, f32[24,4]{0,1:T(4,128)S(1)} %add_rsqrt_fusion, ...), kind=kOutput, calls=%fused_computation.11 | convolution fusion | flops 101099520 | bytes 4854276 | tf_op jit(solution)/shard_map/shj,hjd->sd/dot_general | solution.py:80
  139.1 0.6 copy.38
  139.7 0.6 dynamic-slice
  141.0 58.7 %all-gather.6.cloned.1.call-done = f32[384,4096]{1,0:T(8,128)} async-done(((f32[24,4096]{1,0:T(8,128)}), f32[384,4096]{1,0:T(8,128)}) %all-gather.6.cloned.1.call-update) | async-done | bytes 6291472 | tf_op jit(solution)/shard_map/all_gather | solution.py:84
  199.7 3.1 %reduce_sum.66 = f32[24,4096]{1,0:T(8,128)S(1)} reduce(f32[16,24,4096]{2,1,0:T(8,128)} %bitcast.64, f32[]{:T(128)} %constant.14.clone.1), dimensions={0}, to_apply=%region_4.5 | reduce | flops 1474560 | bytes 6684676 | tf_op jit(solution)/shard_map/reduce_sum | solution.py:85
  203.0 8.3 %fusion.50 = (f32[24]{0:T(128)S(1)}, f32[24,1572]{1,0:T(8,128)S(1)}) fusion(bf16[1572,4096]{1,0:T(8,128)(2,1)} %param.29, bf16[24,4096]{1,0:T(8,128)(2,1)S(1)} %get-tuple-element.84, f32[4096]{0:T(1024)S(1)} %copy-done.4, f32[24]{0:T(128)S(1)} %add_rsqrt_fusion.1), kind=kOutput, calls=%fused_computation.74 | convolution fusion | flops 309498688 | bytes 13241920 | tf_op jit(solution)/shard_map/sd,vd->sv/dot_general | solution.py:88
  212.2 31.8 %all-reduce.3 = (f32[384]{0:T(512)S(1)}, f32[384]{0:T(512)S(1)}, f32[384]{0:T(512)S(1)}) all-reduce(f32[384]{0:T(512)S(1)} %dynamic-update-slice, f32[384]{0:T(512)S(1)} %dynamic-update-slice.1, f32[384]{0:T(512)S(1)} %dynamic-update-slice.2), channel_id=3, replica_groups=mesh['groups'=2,'row'=8,'head'=2] {'row','head'}, use_global_device_ids=true, to_apply=%add | all-reduce | flops 1152 | bytes 9216
  244.2 0.6 constant_dynamic-slice_fusion.3
  245.1 0.6 while.14
  245.7 0.5 add_subtract_fusion
  (64 shorter events, 2.7 us)
Async XLA Ops:
  7.2 128.0 %copy-start = (bf16[4,64,4096]{2,1,0:T(8,128)(2,1)S(1)}, bf16[4,64,4096]{2,1,0:T(8,128)(2,1)}, u32[]{:S(2)}) copy-start(bf16[4,64,4096]{2,1,0:T(8,128)(2,1)} %param.24) | copy-start | bytes 6291460
  7.2 125.9 %all-reduce.6.cloned.1.call-start = ((), (), s32[]{:S(2)}) async-start(), calls=%async_computation | async-start | bytes 393216 | tf_op jit(solution)/shard_map/psum | solution.py:71
  46.6 7.9 %copy-start.5 = (f32[24,4]{0,1:T(4,128)}, f32[24,4]{0,1:T(4,128)S(1)}, u32[]{:S(2)}) copy-start(f32[24,4]{0,1:T(4,128)S(1)} %get-tuple-element.88) | copy-start | bytes 1156
  54.5 2.7 %copy-start.1 = (f32[24,4,32,512]{3,2,1,0:T(8,128)}, f32[24,4,32,512]{3,2,1,0:T(8,128)S(1)}, u32[]{:S(2)}) copy-start(f32[24,4,32,512]{3,2,1,0:T(8,128)S(1)} %multiply_add_fusion) | copy-start | bytes 18874372
  57.2 78.0 %copy-start.2 = (bf16[24,4096]{1,0:T(8,128)(2,1)S(1)}, bf16[24,4096]{1,0:T(8,128)(2,1)}, u32[]{:S(2)}) copy-start(bf16[24,4096]{1,0:T(8,128)(2,1)} %param.18) | copy-start | bytes 589828
  57.2 78.0 %copy-start.3 = (f32[4096]{0:T(1024)S(1)}, f32[4096]{0:T(1024)}, u32[]{:S(2)}) copy-start(f32[4096]{0:T(1024)} %param.19) | copy-start | bytes 49156
  57.2 78.0 %copy-start.6 = (f32[4,64]{1,0:T(4,128)S(1)}, f32[4,64]{1,0:T(4,128)}, u32[]{:S(2)}) copy-start(f32[4,64]{1,0:T(4,128)} %param.27) | copy-start | bytes 3076
  57.2 82.5 %copy-start.8 = (u32[32]{0:T(128)S(1)}, u32[32]{0:T(128)}, u32[]{:S(2)}) copy-start(u32[32]{0:T(128)} %constant.57) | copy-start | bytes 388
  57.2 83.7 %copy-start.7 = (s32[24]{0:T(128)S(1)}, s32[24]{0:T(128)}, u32[]{:S(2)}) copy-start(s32[24]{0:T(128)} %param.33) | copy-start | bytes 292
  61.1 138.6 %all-gather.6.cloned.1.call-start = ((), (), s32[]{:S(2)}) async-start(), calls=%async_computation.1 | async-start | bytes 6684672 | tf_op jit(solution)/shard_map/all_gather | solution.py:84
  135.2 67.7 %copy-start.4 = (f32[4096]{0:T(1024)S(1)}, f32[4096]{0:T(1024)}, u32[]{:S(2)}) copy-start(f32[4096]{0:T(1024)} %param.28) | copy-start | bytes 49156
Sparse Core Ops, SparseCore 0:
  61.2 71.7 all-reduce.5
  139.2 60.4 all-gather.5
